TPU v7x, 256 devices: a whole 4x4x8 slice. The times are simulated.
256 devices in a mesh: seq: 128 (over x, y, z_lo, core), fsdp: 2 (over z_hi).
Axes of the slice: x: 4, y: 4, z: 8 (z_hi: 2, z_lo: 4; z = z_hi * 4 + z_lo), core: 2. Of those that a mesh axis runs over, the one named last changes fastest.
Arguments:
- queries: bfloat16 [65536, 2048], P(('seq', 'fsdp')), may hold values from -150 to 150
- key_rotated_rows: bfloat16 [65536, 1024], P(('seq', 'fsdp')), may hold values from -5 to 5
- values: bfloat16 [65536, 1024], P(('seq', 'fsdp')), may hold values from -6 to 6
- out_weight: bfloat16 [2048, 5376], P('seq', 'fsdp'), may hold values from -0.125 to 0.125
- residual: bfloat16 [65536, 5376], P(('seq', 'fsdp')), may hold values from -6 to 6
- norm_gain: float32 [5376], replicated, may hold values from 0.25 to 1.75
- doc_lengths: int32 [64], replicated, may hold values from 1 to 2048, 65536 in all
Outputs:
- output: bfloat16 [65536, 5376], P(('seq', 'fsdp'))
All inputs are finite; a program needn't handle non-finite values.
Results may differ from a plain program's by a relative error of at most 0.007.
Values may be sent and summed in bfloat16 or wider, within the bound.
A program may use at most 128 MiB of HBM per device.

v0:
```python
import jax
import jax.numpy as jnp
from jax import lax
from jax.sharding import PartitionSpec as P

QUERY_HEADS = 16
KEY_VALUE_HEADS = 8
HEAD_SIZE = 128
WINDOW_TOKENS = 1024
QSCALE = 168


def from_behind(value, axis, by):
    count = lax.axis_size(axis)
    pairs = [(i, i + by) for i in range(count) if 0 <= i + by < count]
    return lax.ppermute(value, axis, pairs)


def doc_index(positions, starts):
    return jnp.sum((starts[None, :] <= positions[:, None]).astype(jnp.int32), axis=1) - 1


def shards(queries, key_rotated_rows, values, out_weight, residual, norm_gain, doc_lengths):
    token_rows = queries.shape[0]
    behind = WINDOW_TOKENS // token_rows
    queries_per_group = QUERY_HEADS // KEY_VALUE_HEADS
    scaling = QSCALE ** (-0.5)
    token_offset = lax.axis_index(("seq", "fsdp")) * token_rows
    starts = jnp.cumsum(doc_lengths) - doc_lengths
    earlier = [
        from_behind((key_rotated_rows, values), ("seq", "fsdp"), distance)
        for distance in range(1, behind + 1)
    ]
    ordered = earlier[::-1] + [(key_rotated_rows, values)]
    key_gathered = jnp.concatenate([paired[0] for paired in ordered], axis=0)
    value_gathered = jnp.concatenate([paired[1] for paired in ordered], axis=0)
    total_count = key_gathered.shape[0]
    q_pos = token_offset + jnp.arange(token_rows, dtype=jnp.int32)
    k_pos = token_offset - behind * token_rows + jnp.arange(total_count, dtype=jnp.int32)
    q_doc = doc_index(q_pos, starts)
    k_doc = doc_index(k_pos, starts)
    lag = q_pos[:, None] - k_pos[None, :]
    allowed = (
        (q_doc[:, None] == k_doc[None, :])
        & (lag >= 0)
        & (lag < WINDOW_TOKENS)
        & (k_pos[None, :] >= 0)
    )
    last_pos = k_pos[token_rows - 1 :: token_rows]
    live = (last_pos >= 0) & (doc_index(last_pos, starts) == q_doc[0])
    live = jnp.concatenate([live[:-1], jnp.ones((1,), dtype=bool)])
    query_head_rows = queries.reshape(
        token_rows, KEY_VALUE_HEADS, queries_per_group * HEAD_SIZE
    ).transpose(1, 0, 2)
    key_head_rows = key_gathered.reshape(total_count, KEY_VALUE_HEADS, HEAD_SIZE).transpose(1, 0, 2)
    value_head_rows = value_gathered.reshape(total_count, KEY_VALUE_HEADS, HEAD_SIZE).transpose(
        1, 0, 2
    )

    def attend(operands):
        q_head, k_head, v_head = operands
        q_head = q_head.reshape(token_rows, queries_per_group, HEAD_SIZE)
        scores = jnp.einsum("qgd,kd->gqk", q_head, k_head, preferred_element_type=jnp.float32)
        scores = jnp.where(allowed[None], scores * scaling, -jnp.inf)
        peak = jnp.max(scores, axis=-1, keepdims=True)
        expon = jnp.exp(scores - peak)
        probs = (expon / jnp.sum(expon, axis=-1, keepdims=True)).astype(jnp.bfloat16)
        mixed = jnp.einsum("gqk,kd->qgd", probs, v_head, preferred_element_type=jnp.float32)
        return mixed.reshape(token_rows, queries_per_group * HEAD_SIZE)

    heads_out = lax.map(attend, (query_head_rows, key_head_rows, value_head_rows))
    attended = (
        heads_out.transpose(1, 0, 2)
        .reshape(token_rows, QUERY_HEADS * HEAD_SIZE)
        .astype(jnp.bfloat16)
    )
    widened = lax.all_gather(out_weight, "fsdp", axis=1, tiled=True)
    projected = jnp.dot(
        attended,
        lax.all_gather(widened, "seq", axis=0, tiled=True),
        preferred_element_type=jnp.float32,
    )
    meansq = jnp.mean(projected * projected, axis=-1, keepdims=True)
    output = residual.astype(jnp.float32) + norm_gain * projected * lax.rsqrt(meansq + 1e-06)
    return output.astype(jnp.bfloat16)


def solution(mesh):
    in_specs = (
        P(("seq", "fsdp"), None),
        P(("seq", "fsdp"), None),
        P(("seq", "fsdp"), None),
        P("seq", "fsdp"),
        P(("seq", "fsdp"), None),
        P(),
        P(),
    )
    out_specs = P(("seq", "fsdp"), None)
    return jax.shard_map(shards, mesh=mesh, in_specs=in_specs, out_specs=out_specs, check_vma=False)
```

profile of v0, /device:TPU:1, one launch (start us, length us, event | category | flops | bytes accessed | tf_op | source)
XLA Modules:
  0.0 375.2 jit_solution(17282260922316377553)
XLA Ops:
  6.5 12.5 %all_gather.6 = bf16[16,5376]{1,0:T(8,128)(2,1)} all-gather(bf16[16,2688]{1,0:T(8,128)(2,1)} %param.12), channel_id=1, replica_groups=mesh['seq'=128,'fsdp'=2] {'fsdp'}, dimensions={1}, use_global_device_ids=true | all-gather | bytes 258048 | tf_op jit(solution)/shard_map/all_gather | solution.py:77
  19.0 2.7 collective-permute-start
  21.7 8.0 %collective-permute-start.1 = (bf16[256,1024]{1,0:T(8,128)(2,1)}, bf16[256,1024]{1,0:T(8,128)(2,1)}, u32[]{:S(2)}, u32[]{:S(2)}) collective-permute-start(bf16[256,1024]{1,0:T(8,128)(2,1)} %param.11), channel_id=1, source_target_pairs={{0,3},{1,4},{2,5},{3,6},{4,7},{5,8},{6,9},{7,10},{8,11},{9,12},{10... | collective-permute-start | bytes 1572872 | tf_op jit(solution)/shard_map/ppermute | solution.py:16
  29.7 1.9 collective-permute-start.2
  31.6 4.0 %collective-permute-start.3 = (bf16[256,1024]{1,0:T(8,128)(2,1)}, bf16[256,1024]{1,0:T(8,128)(2,1)}, u32[]{:S(2)}, u32[]{:S(2)}) collective-permute-start(bf16[256,1024]{1,0:T(8,128)(2,1)} %param.11), channel_id=1, source_target_pairs={{0,1},{1,2},{2,3},{3,4},{4,5},{5,6},{6,7},{7,8},{8,9},{9,10},{10,1... | collective-permute-start | bytes 1572872 | tf_op jit(solution)/shard_map/ppermute | solution.py:16
  36.9 4.6 %collective-permute-start.4 = (bf16[256,1024]{0,1:T(8,128)(2,1)S(1)}, bf16[256,1024]{0,1:T(8,128)(2,1)}, u32[]{:S(2)}, u32[]{:S(2)}) collective-permute-start(bf16[256,1024]{0,1:T(8,128)(2,1)S(1)} %copy.25), channel_id=1, source_target_pairs={{0,4},{1,5},{2,6},{3,7},{4,8},{5,9},{6,10},{7,11},{8,12},{9,13},{1... | collective-permute-start | bytes 1572872 | tf_op jit(solution)/shard_map/ppermute | solution.py:16
  43.4 2.3 copy.30
  46.5 6.1 %collective-permute-start.5 = (bf16[256,1024]{0,1:T(8,128)(2,1)S(1)}, bf16[256,1024]{0,1:T(8,128)(2,1)}, u32[]{:S(2)}, u32[]{:S(2)}) collective-permute-start(bf16[256,1024]{0,1:T(8,128)(2,1)S(1)} %copy.25), channel_id=1, source_target_pairs={{0,3},{1,4},{2,5},{3,6},{4,7},{5,8},{6,9},{7,10},{8,11},{9,12},{10... | collective-permute-start | bytes 1572872 | tf_op jit(solution)/shard_map/ppermute | solution.py:16
  53.8 35.7 %collective-permute-start.6 = (bf16[256,1024]{0,1:T(8,128)(2,1)S(1)}, bf16[256,1024]{0,1:T(8,128)(2,1)}, u32[]{:S(2)}, u32[]{:S(2)}) collective-permute-start(bf16[256,1024]{0,1:T(8,128)(2,1)S(1)} %copy.25), channel_id=1, source_target_pairs={{0,2},{1,3},{2,4},{3,5},{4,6},{5,7},{6,8},{7,9},{8,10},{9,11},{10,... | collective-permute-start | bytes 1572872 | tf_op jit(solution)/shard_map/ppermute | solution.py:16
  90.6 1.9 collective-permute-start.7
  94.7 2.7 copy.24
  101.8 5.5 %collective-permute-done.7 = bf16[256,1024]{0,1:T(8,128)(2,1)} collective-permute-done((bf16[256,1024]{0,1:T(8,128)(2,1)S(1)}, bf16[256,1024]{0,1:T(8,128)(2,1)}, u32[]{:S(2)}, u32[]{:S(2)}) %collective-permute-start.7) | collective-permute-done | bytes 524320 | tf_op jit(solution)/shard_map/ppermute | solution.py:16
  109.9 51.1 %while.11 = (s32[]{:T(128)}, bf16[8,256,256]{1,2,0:T(8,128)(2,1)S(1)}, bf16[8,1280,128]{1,2,0:T(8,128)(2,1)}, bf16[8,1280,128]{1,2,0:T(8,128)(2,1)}, bf16[8,256,...) while((s32[]{:T(128)}, ...), condition=%wide.region_6.7_spmd.clone, body=%wide.region_3.6_spmd.clone.sunk | while | flops 511511552 | bytes 2902901 | solution.py:71
  111.9 2.0 fusion.57
  113.9 2.3 fusion.58
  118.3 2.0 fusion.57
  120.3 2.3 fusion.58
  124.7 2.0 fusion.57
  126.6 2.3 fusion.58
  131.1 2.0 fusion.57
  133.0 2.3 fusion.58
  137.4 2.0 fusion.57
  139.4 2.3 fusion.58
  143.8 2.0 fusion.57
  145.8 2.3 fusion.58
  150.2 2.0 fusion.57
  152.2 2.4 fusion.58
  156.6 2.0 fusion.57
  158.6 2.3 fusion.58
  161.0 193.7 %all-gather.2.cloned.1.call-done = bf16[2048,5376]{1,0:T(8,128)(2,1)} async-done(((bf16[16,5376]{1,0:T(8,128)(2,1)}), bf16[2048,5376]{1,0:T(8,128)(2,1)}) %all-gather.2.cloned.1.call-update) | async-done | bytes 22020112 | tf_op jit(solution)/shard_map/all_gather | solution.py:80
  354.7 11.0 %multiply_reduce_fusion = (f32[256]{0:T(256)S(1)}, f32[256,5376]{1,0:T(8,128)S(1)}) fusion(bf16[256,2048]{0,1:T(8,128)(2,1)S(1)} %bitcast.77, bf16[2048,5376]{1,0:T(8,128)(2,1)} %all-gather.2.cloned.1.call-done), kind=kOutput, calls=%fused_computation.29 | convolution fusion | flops 5639897088 | bytes 28574720 | tf_op jit(solution)/shard_map/dot_general | solution.py:78
  365.8 2.5 add_convert_fusion
  (69 shorter events, 31.4 us)
Async XLA Ops:
  6.5 348.2 %all-gather.2.cloned.1.call-start = ((), (), s32[]{:S(2)}) async-start(), calls=%async_computation | async-start | bytes 22192128 | tf_op jit(solution)/shard_map/all_gather | solution.py:80
  19.0 26.7 %collective-permute-start = (bf16[256,1024]{1,0:T(8,128)(2,1)}, bf16[256,1024]{1,0:T(8,128)(2,1)S(1)}, u32[]{:S(2)}, u32[]{:S(2)}) collective-permute-start(bf16[256,1024]{1,0:T(8,128)(2,1)} %param.11), channel_id=1, source_target_pairs={{0,4},{1,5},{2,6},{3,7},{4,8},{5,9},{6,10},{7,11},{8,12},{9,13},{1... | collective-permute-start | bytes 1572872 | tf_op jit(solution)/shard_map/ppermute | solution.py:16
  21.7 32.0 %collective-permute-start.1 = (bf16[256,1024]{1,0:T(8,128)(2,1)}, bf16[256,1024]{1,0:T(8,128)(2,1)}, u32[]{:S(2)}, u32[]{:S(2)}) collective-permute-start(bf16[256,1024]{1,0:T(8,128)(2,1)} %param.11), channel_id=1, source_target_pairs={{0,3},{1,4},{2,5},{3,6},{4,7},{5,8},{6,9},{7,10},{8,11},{9,12},{10... | collective-permute-start | bytes 1572872 | tf_op jit(solution)/shard_map/ppermute | solution.py:16
  29.7 60.9 %collective-permute-start.2 = (bf16[256,1024]{1,0:T(8,128)(2,1)}, bf16[256,1024]{1,0:T(8,128)(2,1)}, u32[]{:S(2)}, u32[]{:S(2)}) collective-permute-start(bf16[256,1024]{1,0:T(8,128)(2,1)} %param.11), channel_id=1, source_target_pairs={{0,2},{1,3},{2,4},{3,5},{4,6},{5,7},{6,8},{7,9},{8,10},{9,11},{10,... | collective-permute-start | bytes 1572872 | tf_op jit(solution)/shard_map/ppermute | solution.py:16
  31.6 62.0 %collective-permute-start.3 = (bf16[256,1024]{1,0:T(8,128)(2,1)}, bf16[256,1024]{1,0:T(8,128)(2,1)}, u32[]{:S(2)}, u32[]{:S(2)}) collective-permute-start(bf16[256,1024]{1,0:T(8,128)(2,1)} %param.11), channel_id=1, source_target_pairs={{0,1},{1,2},{2,3},{3,4},{4,5},{5,6},{6,7},{7,8},{8,9},{9,10},{10,1... | collective-permute-start | bytes 1572872 | tf_op jit(solution)/shard_map/ppermute | solution.py:16
  36.9 60.5 %collective-permute-start.4 = (bf16[256,1024]{0,1:T(8,128)(2,1)S(1)}, bf16[256,1024]{0,1:T(8,128)(2,1)}, u32[]{:S(2)}, u32[]{:S(2)}) collective-permute-start(bf16[256,1024]{0,1:T(8,128)(2,1)S(1)} %copy.25), channel_id=1, source_target_pairs={{0,4},{1,5},{2,6},{3,7},{4,8},{5,9},{6,10},{7,11},{8,12},{9,13},{1... | collective-permute-start | bytes 1572872 | tf_op jit(solution)/shard_map/ppermute | solution.py:16
  45.7 49.0 %copy-start.2 = (bf16[256,1024]{1,0:T(8,128)(2,1)S(1)}, bf16[256,1024]{1,0:T(8,128)(2,1)}, u32[]{:S(2)}) copy-start(bf16[256,1024]{1,0:T(8,128)(2,1)} %param.11) | copy-start | bytes 1572868
  45.7 0.8 copy-start.3
  46.5 52.1 %collective-permute-start.5 = (bf16[256,1024]{0,1:T(8,128)(2,1)S(1)}, bf16[256,1024]{0,1:T(8,128)(2,1)}, u32[]{:S(2)}, u32[]{:S(2)}) collective-permute-start(bf16[256,1024]{0,1:T(8,128)(2,1)S(1)} %copy.25), channel_id=1, source_target_pairs={{0,3},{1,4},{2,5},{3,6},{4,7},{5,8},{6,9},{7,10},{8,11},{9,12},{10... | collective-permute-start | bytes 1572872 | tf_op jit(solution)/shard_map/ppermute | solution.py:16
  53.8 46.9 %collective-permute-start.6 = (bf16[256,1024]{0,1:T(8,128)(2,1)S(1)}, bf16[256,1024]{0,1:T(8,128)(2,1)}, u32[]{:S(2)}, u32[]{:S(2)}) collective-permute-start(bf16[256,1024]{0,1:T(8,128)(2,1)S(1)} %copy.25), channel_id=1, source_target_pairs={{0,2},{1,3},{2,4},{3,5},{4,6},{5,7},{6,8},{7,9},{8,10},{9,11},{10,... | collective-permute-start | bytes 1572872 | tf_op jit(solution)/shard_map/ppermute | solution.py:16
  90.6 16.7 %collective-permute-start.7 = (bf16[256,1024]{0,1:T(8,128)(2,1)S(1)}, bf16[256,1024]{0,1:T(8,128)(2,1)}, u32[]{:S(2)}, u32[]{:S(2)}) collective-permute-start(bf16[256,1024]{0,1:T(8,128)(2,1)S(1)} %copy.25), channel_id=1, source_target_pairs={{0,1},{1,2},{2,3},{3,4},{4,5},{5,6},{6,7},{7,8},{8,9},{9,10},{10,1... | collective-permute-start | bytes 1572872 | tf_op jit(solution)/shard_map/ppermute | solution.py:16
  97.4 12.5 %copy-start.1 = (bf16[8,256,256]{1,2,0:T(8,128)(2,1)S(1)}, bf16[8,256,256]{1,2,0:T(8,128)(2,1)}, u32[]{:S(2)}) copy-start(bf16[8,256,256]{1,2,0:T(8,128)(2,1)} %custom-call.2) | copy-start | bytes 3145732
  108.4 1.5 copy-start.4
  354.7 11.0 %copy-start = (bf16[256,5376]{1,0:T(8,128)(2,1)S(1)}, bf16[256,5376]{1,0:T(8,128)(2,1)}, u32[]{:S(2)}) copy-start(bf16[256,5376]{1,0:T(8,128)(2,1)} %param.13) | copy-start | bytes 8257540
  354.7 11.0 %copy-start.5 = (f32[5376]{0:T(1024)S(1)}, f32[5376]{0:T(1024)}, u32[]{:S(2)}) copy-start(f32[5376]{0:T(1024)} %param.14) | copy-start | bytes 64516
Sparse Core Ops, SparseCore 0:
  19.1 335.5 all-gather.1
where the time goes:
time: 377 us; the launch traced here: 375 us
  waiting for transfers between devices  200 us (53%)
  starting transfers between devices  65 us (17%)
  matrix products  45.5 us (12%)
  local copies, waits for them, and re-layouts  25.6 us (7%)
  between operations  13.6 us (4%)
  blocking collectives  12.5 us (3%)
  other arithmetic  12.4 us (3%)
    all_gather x1, waiting for transfers between devices, shards(): lax.all_gather(widened, 'seq', axis=0, tiled=True)  194 us
    ppermute x8, starting transfers between devices, from_behind(): return lax.ppermute(value, axis, pairs)  65 us
    dot_general x8, matrix products, attend(): jnp.einsum('gqk,kd->qgd', probs, v_head, preferred_element_type=jnp.float32)  18.7 us
    sub x8, matrix products, attend(): expon = jnp.exp(scores - peak)  15.8 us
    unnamed x22, local copies, waits for them, and re-layouts  14.6 us
    all_gather x1, blocking collectives, shards(): widened = lax.all_gather(out_weight, 'fsdp', axis=1, tiled=True)  12.5 us
    dot_general x1, matrix products, shards(): jnp.dot(attended, lax.all_gather(widened, 'seq', axis=0, tiled=True), pre...  11 us
    and x8, other arithmetic, shards(): (q_doc[:, None] == k_doc[None, :]) & (lag >= 0) & (lag < WINDOW_TOKENS)  8.73 us
  transfers between devices with their start and end apart: 9, of which 3 were waited for; matrix products, arithmetic and copies ran while one was open for 18% of the time, Pallas kernels for 0%

commit v1 on v0

v1 whole, which is shorter than its diff:
```python
import functools
import math

import jax
import jax.numpy as jnp
from jax import lax
from jax.experimental import pallas as pl
from jax.experimental.pallas import tpu as pltpu
from jax.sharding import PartitionSpec as P

QUERY_HEADS = 16
KEY_VALUE_HEADS = 8
HEAD_SIZE = 128
WINDOW = 1024
QSCALE = 168
ROWS = 256
D = 5376
HALF = D // 2
CHUNKS = 4
CHUNK_COLS = KEY_VALUE_HEADS * HEAD_SIZE // CHUNKS
STAGES = 8
TICKS = STAGES + 4
MESH = pl.DeviceIdType.MESH


def coordinates():
    s = lax.axis_index("seq")
    zh = lax.axis_index("fsdp")
    core = s % 2
    zl = (s // 2) % 4
    y = (s // 8) % 4
    x = s // 32
    return s, zh, core, zl, y, x


def comm_kernel(
    k_ref, v_ref, w_ref, kb, vb, wb,
    local_sem, zs, zr, fs, fr, ss, sr, ds, dr, kvs, kvr,
):
    s, zh, core, zl, y, x = coordinates()
    z = zh * 4 + zl
    f = x + core * (y - x)
    g = y + core * (x - y)
    f_stride = 32 - 24 * core
    g_stride = 8 + 24 * core

    def device(seq, fsdp):
        return {"seq": seq, "fsdp": fsdp}

    def at_z(step):
        to = (z + step + 8) % 8
        return device(s + 2 * (to % 4 - zl), to // 4)

    def at_f(step):
        return device(s + f_stride * ((f + step + 4) % 4 - f), zh)

    def at_g(step):
        return device(s + g_stride * ((g + step + 4) % 4 - g), zh)

    def at_pair(step, fsdp, to_core):
        return device((s - core + 2 * step + 128) % 128 + to_core, fsdp)

    partner = device(s + 1 - 2 * core, zh)

    barrier = pltpu.get_barrier_semaphore()
    known = [at_z(1), at_z(-1), at_f(1), at_f(-1), at_g(1), at_g(-1), partner]
    for step in (-1, 1):
        for fsdp in (0, 1):
            for to_core in (0, 1):
                known.append(at_pair(step, fsdp, to_core))
    for to_core in (0, 1):
        known.append(at_pair(0, 1 - zh, to_core))
    for who in known:
        pl.semaphore_signal(barrier, inc=1, device_id=who, device_id_type=MESH)
    own = pltpu.make_async_copy(w_ref, wb.at[core, z, g, f], local_sem)
    own.start()
    pl.semaphore_wait(barrier, len(known))

    def remote(src, dst, send, recv, who):
        return pltpu.make_async_remote_copy(
            src_ref=src, dst_ref=dst, send_sem=send, recv_sem=recv, device_id=who, device_id_type=MESH
        )

    def cols(chunk):
        return pl.ds(pl.multiple_of(chunk * CHUNK_COLS, CHUNK_COLS), CHUNK_COLS)

    def kv_pair(src, slot, chunk, send_row, who):
        out = []
        for n, (mine, buf) in enumerate(((k_ref, kb), (v_ref, vb))):
            source = mine.at[:, cols(chunk)] if src is None else buf.at[src, :, cols(chunk)]
            out.append(
                remote(source, buf.at[slot, :, cols(chunk)], kvs.at[send_row, chunk, n], kvr.at[slot, chunk, n], who)
            )
        return out

    def start(copies):
        for copy in copies:
            copy.start()

    def arrived(slot, chunk):
        for copy in kv_pair(slot, slot, chunk, 0, partner):
            copy.wait_recv()

    is_a = zh == 0
    first = core == 0
    has_opposite = jnp.logical_not(jnp.logical_and(is_a, first))
    has_three = jnp.logical_not(jnp.logical_and(zh == 1, core == 1))
    opposite_core = core * zh
    three_core = jnp.where(first, 1, 0)
    three_step = jnp.where(first, -1, 0)

    def route0(chunk):
        return kv_pair(None, 0, chunk, 0, at_pair(1, zh, core))

    def route1(chunk):
        return kv_pair(None, 1, chunk, 1, at_pair(1, 1 - zh, opposite_core))

    def route2_own(chunk):
        return kv_pair(None, 2, chunk, 2, partner)

    def route2_relay(chunk):
        return kv_pair(0, 2, chunk, 2, partner)

    def route3(chunk):
        return kv_pair(1, 3, chunk, 3, at_pair(three_step, zh, three_core))

    def route4_a(chunk):
        return kv_pair(0, 3, chunk, 4, at_pair(-1, 1, 0))

    def route4_b(chunk):
        return kv_pair(3, 1, chunk, 4, partner)

    def kv_begin(chunk, _):
        start(route0(chunk))

        @pl.when(has_opposite)
        def _():
            start(route1(chunk))

        @pl.when(first)
        def _():
            start(route2_own(chunk))

        return 0

    def kv_relay_near(chunk):
        arrived(0, chunk)

        @pl.when(core == 1)
        def _():
            start(route2_relay(chunk))

        @pl.when(jnp.logical_and(is_a, first))
        def _():
            start(route4_a(chunk))

    def kv_relay_far(chunk):
        @pl.when(has_three)
        def _():
            arrived(1, chunk)
            start(route3(chunk))

    def kv_relay_last(chunk):
        arrived(3, chunk)

        @pl.when(jnp.logical_and(zh == 1, first))
        def _():
            start(route4_b(chunk))

    def kv_finish(chunk):
        arrived(2, chunk)

        @pl.when(jnp.logical_not(has_three))
        def _():
            arrived(1, chunk)

    def piece(i):
        return (z + ((i + 1) // 2) * (1 - 2 * (i % 2)) + 8) % 8

    def z_send(src_piece, to_stage, step):
        ref = wb.at[core, src_piece, g, f]
        return remote(ref, ref, zs.at[to_stage], zr.at[to_stage], at_z(step))

    def z_recv(i):
        ref = wb.at[core, piece(i), g, f]
        return remote(ref, ref, zs.at[i], zr.at[i], partner)

    def f_copy(i, from_f, lane, step):
        ref = wb.at[core, piece(i), g, (from_f + 4) % 4]
        return remote(ref, ref, fs.at[i, lane], fr.at[i, lane], at_f(step))

    def s_copy(i, from_g, lane, step):
        ref = wb.at[core, piece(i), (from_g + 4) % 4]
        return remote(ref, ref, ss.at[i, lane], sr.at[i, lane], at_g(step))

    def s_half(i, from_g, lane, step):
        ref = wb.at[core, piece(i), (from_g + 4) % 4, pl.ds(2 * (lane - 2), 2)]
        return remote(ref, ref, ss.at[i, lane], sr.at[i, lane], at_g(step))

    def d_copy(i, from_core):
        ref = wb.at[from_core, piece(i)]
        return remote(ref, ref, ds.at[i], dr.at[i], partner)

    def forward_sign(i):
        return 1 - 2 * (i % 2)

    own.wait()
    lax.fori_loop(0, 1, kv_begin, 0)

    def tick(t, _):
        @pl.when(t == 0)
        def _():
            z_send(z, 1, 1).start()
            z_send(z, 2, -1).start()

        @pl.when(jnp.logical_and(t > 0, t < STAGES))
        def _():
            z_recv(t).wait_recv()

            @pl.when((t <= 4) | ((t == 5) & (core == 0)) | ((t == 6) & (core == 1)))
            def _():
                to_stage = jnp.minimum(t + 2, 7)
                z_send(piece(t), to_stage, 2 * (t % 2) - 1).start()

        @pl.when(t < STAGES)
        def _():
            f_copy(t, f, 0, 1).start()
            f_copy(t, f, 1, -1).start()

        @pl.when((t >= 1) & (t < STAGES + 1))
        def _():
            i = t - 1
            f_copy(i, f - 1, 0, 1).wait_recv()
            f_copy(i, f + 1, 1, -1).wait_recv()
            sign = forward_sign(i)
            f_copy(i, f - sign, 2, sign).start()

        @pl.when((t >= 2) & (t < STAGES + 2))
        def _():
            i = t - 2
            f_copy(i, f + 2, 2, 1).wait_recv()
            s_copy(i, g, 0, 1).start()
            s_copy(i, g, 1, -1).start()

        @pl.when((t >= 3) & (t < STAGES + 3))
        def _():
            i = t - 3
            s_copy(i, g - 1, 0, 1).wait_recv()
            s_copy(i, g + 1, 1, -1).wait_recv()
            s_half(i, g - 1, 2, 1).start()
            s_half(i, g + 1, 3, -1).start()

        @pl.when((t >= 4) & (t < STAGES + 4))
        def _():
            i = t - 4
            s_half(i, g + 2, 2, 1).wait_recv()
            s_half(i, g + 2, 3, -1).wait_recv()
            d_copy(i, core).start()

        @pl.when((t >= 1) & (t < CHUNKS))
        def _():
            kv_begin(t, 0)

        @pl.when((t >= 2) & (t < 2 + 2 * CHUNKS) & (t % 2 == 0))
        def _():
            chunk = (t - 2) // 2
            kv_relay_near(chunk)
            kv_relay_far(chunk)

        @pl.when((t >= 4) & (t < 4 + 2 * CHUNKS) & (t % 2 == 0))
        def _():
            chunk = (t - 4) // 2
            kv_relay_last(chunk)

        return 0

    lax.fori_loop(0, TICKS, tick, 0)

    def finish_kv(chunk, _):
        kv_finish(chunk)
        for copy in route0(chunk):
            copy.wait_send()

        @pl.when(has_opposite)
        def _():
            for copy in route1(chunk):
                copy.wait_send()

        for copy in route2_own(chunk):
            copy.wait_send()

        @pl.when(has_three)
        def _():
            for copy in route3(chunk):
                copy.wait_send()

        @pl.when(first)
        def _():
            for copy in route4_b(chunk):
                copy.wait_send()

        return 0

    lax.fori_loop(0, CHUNKS, finish_kv, 0)

    def finish_w(i, _):
        d_copy(i, 1 - core).wait_recv()
        d_copy(i, core).wait_send()
        f_copy(i, f, 0, 1).wait_send()
        f_copy(i, f, 1, 1).wait_send()
        f_copy(i, f, 2, 1).wait_send()
        s_copy(i, g, 0, 1).wait_send()
        s_copy(i, g, 1, 1).wait_send()
        s_half(i, g, 2, 1).wait_send()
        s_half(i, g, 3, 1).wait_send()

        @pl.when(i > 0)
        def _():
            z_recv(i).wait_send()

        return 0

    lax.fori_loop(0, STAGES, finish_w, 0)


def communicate(keys, values, weight):
    anyspace = pl.BlockSpec(memory_space=pl.ANY)
    dma = pltpu.SemaphoreType.DMA
    return pl.pallas_call(
        comm_kernel,
        out_shape=(
            jax.ShapeDtypeStruct((4, ROWS, 1024), jnp.bfloat16),
            jax.ShapeDtypeStruct((4, ROWS, 1024), jnp.bfloat16),
            jax.ShapeDtypeStruct((2, 8, 4, 4, 16, HALF), jnp.bfloat16),
        ),
        in_specs=[anyspace, anyspace, pl.BlockSpec(memory_space=pltpu.VMEM)],
        out_specs=(anyspace, anyspace, anyspace),
        scratch_shapes=[
            dma,
            dma((8,)), dma((8,)),
            dma((8, 3)), dma((8, 3)),
            dma((8, 4)), dma((8, 4)),
            dma((8,)), dma((8,)),
            dma((5, CHUNKS, 2)), dma((4, CHUNKS, 2)),
        ],
        compiler_params=pltpu.CompilerParams(collective_id=0, has_side_effects=True),
        name="exchange",
    )(keys, values, weight)


def low_bound(lengths, offset):
    row = lax.broadcasted_iota(jnp.int32, (64, 64), 0)
    col = lax.broadcasted_iota(jnp.int32, (64, 64), 1)
    starts_col = jnp.sum(jnp.where(col < row, lengths, 0), axis=1, keepdims=True)
    starts = jnp.sum(jnp.where(row == col, starts_col, 0), axis=0, keepdims=True)
    i = lax.broadcasted_iota(jnp.int32, (ROWS, 1), 0)
    begins = jnp.max(jnp.where(starts <= i + offset, starts, 0), axis=1, keepdims=True)
    return jnp.maximum(begins - offset + WINDOW, i + 1)


def attention_kernel(lengths_ref, q_ref, kb_ref, vb_ref, k_ref, v_ref, o_ref):
    s, zh, _, _, _, _ = coordinates()
    offset = (s * 2 + zh) * ROWS
    low = low_bound(lengths_ref[...], offset)
    factor = math.log2(math.e) * QSCALE ** (-0.5)
    keys = jnp.concatenate([kb_ref[j] for j in range(4)] + [k_ref[...]], axis=0)
    vals = jnp.concatenate([vb_ref[j] for j in range(4)] + [v_ref[...]], axis=0)
    width = WINDOW + 128
    for half in range(2):
        rows = slice(128 * half, 128 * half + 128)
        k_half = keys[128 * half : 128 * half + width]
        v_half = vals[128 * half : 128 * half + width]
        r = lax.broadcasted_iota(jnp.int32, (128, width), 1) + 128 * half
        i = lax.broadcasted_iota(jnp.int32, (128, width), 0) + 128 * half
        allowed = (r >= low[rows]) & (r <= i + WINDOW)
        for head in range(2):
            columns = slice(HEAD_SIZE * head, HEAD_SIZE * head + HEAD_SIZE)
            scores = lax.dot_general(
                q_ref[rows, columns], k_half, (((1,), (1,)), ((), ())), preferred_element_type=jnp.float32
            )
            scores = jnp.where(allowed, scores, -1e30)
            peak = jnp.max(scores, axis=1, keepdims=True)
            expon = jnp.exp2((scores - peak) * factor)
            total = jnp.sum(expon, axis=1, keepdims=True)
            mixed = jnp.dot(expon.astype(jnp.bfloat16), v_half, preferred_element_type=jnp.float32)
            o_ref[rows, columns] = (mixed / total).astype(jnp.bfloat16)


def attention(lengths, queries, kb, vb, keys, values):
    pair = 2 * HEAD_SIZE
    return pl.pallas_call(
        attention_kernel,
        grid=(KEY_VALUE_HEADS,),
        out_shape=jax.ShapeDtypeStruct((ROWS, QUERY_HEADS * HEAD_SIZE), jnp.bfloat16),
        in_specs=[
            pl.BlockSpec((1, 64), lambda h: (0, 0)),
            pl.BlockSpec((ROWS, pair), lambda h: (0, h)),
            pl.BlockSpec((4, ROWS, HEAD_SIZE), lambda h: (0, 0, h)),
            pl.BlockSpec((4, ROWS, HEAD_SIZE), lambda h: (0, 0, h)),
            pl.BlockSpec((ROWS, HEAD_SIZE), lambda h: (0, h)),
            pl.BlockSpec((ROWS, HEAD_SIZE), lambda h: (0, h)),
        ],
        out_specs=pl.BlockSpec((ROWS, pair), lambda h: (0, h)),
        name="attend",
    )(lengths, queries, kb, vb, keys, values)


TILE = 384
TILES = HALF // TILE


def project_kernel(a_ref, w_ref, res_ref, gain_ref, o_ref, acc):
    n = pl.program_id(0)
    slabs = []
    for x in range(4):
        for y in range(4):
            for zl in range(4):
                slabs.append(w_ref[0, zl, y, x])
                slabs.append(w_ref[1, zl, x, y])
    weight = jnp.concatenate(slabs, axis=0)
    acc[n] = jnp.dot(a_ref[...], weight, preferred_element_type=jnp.float32)

    @pl.when(n == 2 * TILES - 1)
    def _():
        def add(m, total):
            part = acc[m]
            return total + jnp.sum(part * part, axis=1, keepdims=True)

        square = lax.fori_loop(0, 2 * TILES, add, jnp.zeros((ROWS, 1), jnp.float32))
        level = lax.rsqrt(square * (1.0 / D) + 1e-06)
        for m in range(2 * TILES):
            columns = slice(TILE * m, TILE * m + TILE)
            normed = gain_ref[:, columns] * acc[m] * level
            o_ref[:, columns] = (res_ref[:, columns].astype(jnp.float32) + normed).astype(jnp.bfloat16)


def project(attended, wb, residual, gain):
    return pl.pallas_call(
        project_kernel,
        grid=(2 * TILES,),
        out_shape=jax.ShapeDtypeStruct((ROWS, D), jnp.bfloat16),
        in_specs=[
            pl.BlockSpec((ROWS, QUERY_HEADS * HEAD_SIZE), lambda n: (0, 0)),
            pl.BlockSpec((2, 4, 4, 4, 16, TILE), lambda n: (0, n // TILES, 0, 0, 0, n % TILES)),
            pl.BlockSpec((ROWS, D), lambda n: (0, 0)),
            pl.BlockSpec((1, D), lambda n: (0, 0)),
        ],
        out_specs=pl.BlockSpec((ROWS, D), lambda n: (0, 0)),
        scratch_shapes=[pltpu.VMEM((2 * TILES, ROWS, TILE), jnp.float32)],
        compiler_params=pltpu.CompilerParams(vmem_limit_bytes=48 * 1024 * 1024),
        name="project",
    )(attended, wb, residual, gain)


def shards(queries, key_rotated_rows, values, out_weight, residual, norm_gain, doc_lengths):
    kb, vb, wb = communicate(key_rotated_rows, values, out_weight)
    attended = attention(doc_lengths.reshape(1, 64), queries, kb, vb, key_rotated_rows, values)
    return project(attended, wb, residual, norm_gain.reshape(1, D))


def solution(mesh):
    rows = P(("seq", "fsdp"), None)
    in_specs = (rows, rows, rows, P("seq", "fsdp"), rows, P(), P())
    return jax.shard_map(shards, mesh=mesh, in_specs=in_specs, out_specs=rows, check_vma=False)
```

time: 377 us -> 164 us (0.44)
  waiting for transfers between devices: 200 us -> 0 us
  Pallas kernels: 0 us -> 162 us
  starting transfers between devices: 65 us -> 0 us
  matrix products: 45.5 us -> 0 us
  local copies, waits for them, and re-layouts: 25.6 us -> 1.25 us
  between operations: 13.6 us -> 0.05 us
  blocking collectives: 12.5 us -> 0 us
  other arithmetic: 12.4 us -> 0 us
    all_gather x1 -> x0, waiting for transfers between devices: 194 us -> none  [shards(): lax.all_gather(widened, 'seq', axis=0, tiled=True)]
    pallas_call x0 -> x3, Pallas kernels: none -> 162 us  [the longest x1 124 us: communicate(): pl.pallas_call(comm_kernel, out_shape=(jax.ShapeDtypeStruct((4, ROWS, 102...]
    ppermute x8 -> x0, starting transfers between devices: 65 us -> none  [from_behind(): return lax.ppermute(value, axis, pairs)]
    dot_general x9 -> x0, matrix products: 29.7 us -> none  [the longest x8 18.7 us: attend(): jnp.einsum('gqk,kd->qgd', probs, v_head, preferred_element_type=jnp.float32)]
    sub x8 -> x0, matrix products: 15.8 us -> none  [attend(): expon = jnp.exp(scores - peak)]
    unnamed x22 -> x6, local copies, waits for them, and re-layouts: 14.6 us -> 1.23 us
    all_gather x1 -> x0, blocking collectives: 12.5 us -> none  [shards(): widened = lax.all_gather(out_weight, 'fsdp', axis=1, tiled=True)]
    and x8 -> x0, other arithmetic: 8.73 us -> none  [shards(): (q_doc[:, None] == k_doc[None, :]) & (lag >= 0) & (lag < WINDOW_TOKENS)]
  transfers between devices with their start and end apart: 9 -> 0, of which waited for: 3 -> 0; matrix products, arithmetic and copies ran while one was open for 18% -> 0% of each run, Pallas kernels for 0% -> 0%
where the time goes in v1:
time: 164 us; the launch traced here: 163 us
  Pallas kernels  162 us (99%)
    pallas_call x1, Pallas kernels, communicate(): pl.pallas_call(comm_kernel, out_shape=(jax.ShapeDtypeStruct((4, ROWS, 102...  124 us
    pallas_call x1, Pallas kernels, project(): pl.pallas_call(project_kernel, grid=(2 * TILES,), out_shape=jax.ShapeDtyp...  20.6 us
    pallas_call x1, Pallas kernels, attention(): pl.pallas_call(attention_kernel, grid=(KEY_VALUE_HEADS,), out_shape=jax.S...  17.4 us

profile of v1, /device:TPU:1, one launch (start us, length us, event | category | flops | bytes accessed | tf_op | source)
XLA Modules:
  0.0 162.8 jit_solution(854294247735951790)
XLA Ops:
  0.0 123.5 %exchange.1 = (bf16[4,256,1024]{2,1,0:T(8,128)(2,1)}, bf16[4,256,1024]{2,1,0:T(8,128)(2,1)}, bf16[2,8,4,4,16,2688]{5,4,3,2,1,0:T(8,128)(2,1)}) custom-call(bf16[256,1024]{1,0:T(8,128)(2,1)} %k_ref.3, bf16[256,1024]{1,0:T(8,128)(2,1)} %v_ref.3, bf16[16,2688]{1,0:T(8,128)(2,1)} %w_ref.1), custom_call_target="tpu_custom_call" | custom-call | tf_op jit(solution)/shard_map/exchange/pallas_call | solution.py:329
  123.5 0.0 copy-start.2
  123.5 0.0 copy-start.1
  123.6 17.4 %attend.1.a_ref = bf16[256,2048]{1,0:T(8,128)(2,1)} custom-call(s32[1,64]{1,0:T(1,128)} %bitcast.1, bf16[256,2048]{1,0:T(8,128)(2,1)} %q_ref.1, bf16[4,256,1024]{2,1,0:T(8,128)(2,1)} %get-tuple-element.8.kb_ref, bf16[4,256,1024]{2,1,0:T(8,128)(2,1)} %get-tuple-element.9.vb_ref, bf16[256,1024]{1,0:T(8,128)(2,1)} %k_ref.3, bf16[256,1024]{1,0:T(8,128)(2,1)} %v_ref.3), custom_call_target="tpu_custom_call" | custom-call | tf_op jit(solution)/shard_map/attend/pallas_call | solution.py:391
  141.0 0.0 copy-done.2
  141.0 0.0 copy-done.1
  141.0 0.0 copy-start
  141.0 1.2 copy-done
  142.2 20.6 %project.1 = bf16[256,5376]{1,0:T(8,128)(2,1)} custom-call(bf16[256,2048]{1,0:T(8,128)(2,1)S(1)} %copy-done, bf16[2,8,4,4,16,2688]{5,4,3,2,1,0:T(8,128)(2,1)} %get-tuple-element.10.w_ref, bf16[256,5376]{1,0:T(8,128)(2,1)S(1)} %copy-done.1, f32[1,5376]{1,0:T(1,128)S(1)} %reshape.7.gain_ref), custom_call_target="tpu_custom_call" | custom-call | tf_op jit(solution)/shard_map/project/pallas_call | solution.py:438
  (1 shorter events, 0.0 us)
Async XLA Ops:
  123.5 17.5 %copy-start.2 = (f32[5376]{0:T(1024)S(1)}, f32[5376]{0:T(1024)}, u32[]{:S(2)}) copy-start(f32[5376]{0:T(1024)} %param.12) | copy-start | bytes 64516
  123.5 17.5 %copy-start.1 = (bf16[256,5376]{1,0:T(8,128)(2,1)S(1)}, bf16[256,5376]{1,0:T(8,128)(2,1)}, u32[]{:S(2)}) copy-start(bf16[256,5376]{1,0:T(8,128)(2,1)} %res_ref.1) | copy-start | bytes 8257540
  141.0 1.2 copy-start

commit v2 on v1

v2 whole, which is shorter than its diff:
```python
import math

import jax
import jax.numpy as jnp
from jax import lax
from jax.experimental import pallas as pl
from jax.experimental.pallas import tpu as pltpu
from jax.sharding import PartitionSpec as P

QUERY_HEADS = 16
KEY_VALUE_HEADS = 8
HEAD_SIZE = 128
WINDOW = 1024
QSCALE = 168
ROWS = 256
D = 5376
HALF = D // 2
CHUNKS = KEY_VALUE_HEADS
STAGES = 8
TICKS = STAGES + 4
MESH = pl.DeviceIdType.MESH
FACTOR = math.log2(math.e) * QSCALE ** (-0.5)


def coordinates():
    s = lax.axis_index("seq")
    zh = lax.axis_index("fsdp")
    core = s % 2
    zl = (s // 2) % 4
    y = (s // 8) % 4
    x = s // 32
    return s, zh, core, zl, y, x


def exchange_kernel(
    lengths_ref, q_hbm, k_ref, v_ref, w_ref, o_ref, wb,
    q_ref, kb, vb, wv, low_ref,
    local_sem, lw, zs, zr, fs, fr, ss, sr, ds, dr, kvs, kvr,
):
    s, zh, core, zl, y, x = coordinates()
    z = zh * 4 + zl
    f = x + core * (y - x)
    g = y + core * (x - y)
    f_stride = 32 - 24 * core
    g_stride = 8 + 24 * core

    def device(seq, fsdp):
        return {"seq": seq, "fsdp": fsdp}

    def at_z(step):
        to = (z + step + 8) % 8
        return device(s + 2 * (to % 4 - zl), to // 4)

    def at_f(step):
        return device(s + f_stride * ((f + step + 4) % 4 - f), zh)

    def at_g(step):
        return device(s + g_stride * ((g + step + 4) % 4 - g), zh)

    def at_pair(step, fsdp, to_core):
        return device((s - core + 2 * step + 128) % 128 + to_core, fsdp)

    partner = device(s + 1 - 2 * core, zh)

    def w_cols(p):
        return pl.ds(pl.multiple_of((p // 4) * HALF, HALF), HALF)

    barrier = pltpu.get_barrier_semaphore()
    known = [at_z(1), at_z(-1), at_f(1), at_f(-1), at_g(1), at_g(-1), partner]
    for step in (-1, 1):
        for fsdp in (0, 1):
            for to_core in (0, 1):
                known.append(at_pair(step, fsdp, to_core))
    for to_core in (0, 1):
        known.append(at_pair(0, 1 - zh, to_core))
    for who in known:
        pl.semaphore_signal(barrier, inc=1, device_id=who, device_id_type=MESH)
    own_rows = pl.ds(WINDOW, ROWS)
    own = [
        pltpu.make_async_copy(w_ref, wv.at[core, zl, g, f, :, w_cols(z)], local_sem.at[0]),
        pltpu.make_async_copy(k_ref, kb.at[own_rows], local_sem.at[1]),
        pltpu.make_async_copy(v_ref, vb.at[own_rows], local_sem.at[2]),
        pltpu.make_async_copy(q_hbm, q_ref, local_sem.at[3]),
    ]
    for copy in own:
        copy.start()
    low_ref[...] = low_bound(lengths_ref[...], (s * 2 + zh) * ROWS)
    for copy in own:
        copy.wait()
    pl.semaphore_wait(barrier, len(known))

    def remote(src, dst, send, recv, who):
        return pltpu.make_async_remote_copy(
            src_ref=src, dst_ref=dst, send_sem=send, recv_sem=recv, device_id=who, device_id_type=MESH
        )

    def cols(chunk):
        return pl.ds(pl.multiple_of(chunk * HEAD_SIZE, HEAD_SIZE), HEAD_SIZE)

    def slot_rows(slot):
        return pl.ds(slot * ROWS, ROWS)

    def kv_pair(src, slot, chunk, send_row, who):
        return [
            remote(
                buf.at[slot_rows(src), cols(chunk)],
                buf.at[slot_rows(slot), cols(chunk)],
                kvs.at[send_row, chunk, n],
                kvr.at[slot, chunk, n],
                who,
            )
            for n, buf in enumerate((kb, vb))
        ]

    def start(copies):
        for copy in copies:
            copy.start()

    def arrived(slot, chunk):
        for copy in kv_pair(slot, slot, chunk, 0, partner):
            copy.wait_recv()

    def sent(send_row, chunk):
        for copy in kv_pair(4, 0, chunk, send_row, partner):
            copy.wait_send()

    first = core == 0
    a_first = jnp.logical_and(zh == 0, first)
    b_first = jnp.logical_and(zh == 1, first)
    a_second = jnp.logical_and(zh == 0, core == 1)
    b_second = jnp.logical_and(zh == 1, core == 1)
    last_of_four = zl == 3
    inner = jnp.logical_or(b_first, a_second)
    outer = jnp.logical_not(inner)
    to_opposite = jnp.logical_or(core == 1, jnp.logical_and(b_first, last_of_four))
    opposite = at_pair(1, 1 - zh, core * zh)

    def kv_begin(chunk):
        start(kv_pair(4, 0, chunk, 0, at_pair(1, zh, core)))

        @pl.when(to_opposite)
        def _():
            start(kv_pair(4, 1, chunk, 1, opposite))

        @pl.when(first)
        def _():
            start(kv_pair(4, 2, chunk, 2, partner))

    def kv_near(chunk):
        arrived(0, chunk)

        @pl.when(first)
        def _():
            start(kv_pair(0, 3, chunk, 3, at_pair(-1, 1 - zh, zh)))

        @pl.when(core == 1)
        def _():
            start(kv_pair(0, 2, chunk, 2, partner))

    def kv_far(chunk):
        @pl.when(a_second)
        def _():
            arrived(1, chunk)
            start(kv_pair(1, 3, chunk, 3, partner))

        @pl.when(b_first)
        def _():
            arrived(1, chunk)
            start(kv_pair(1, 3, chunk, 4, at_pair(-1, 1, 1)))

    def kv_last(chunk):
        @pl.when(inner)
        def _():
            arrived(3, chunk)

        @pl.when(b_first)
        def _():
            start(kv_pair(3, 1, chunk, 5, partner))

        @pl.when(jnp.logical_and(a_second, jnp.logical_not(last_of_four)))
        def _():
            start(kv_pair(3, 1, chunk, 5, at_pair(1, 0, 0)))

    def kv_done(chunk):
        arrived(2, chunk)

        @pl.when(outer)
        def _():
            arrived(1, chunk)
            arrived(3, chunk)

    def attend(head):
        pair = pl.ds(pl.multiple_of(head * 2 * HEAD_SIZE, 2 * HEAD_SIZE), 2 * HEAD_SIZE)
        width = WINDOW + 128
        for half in range(2):
            rows = slice(128 * half, 128 * half + 128)
            span = slice(128 * half, 128 * half + width)
            keys = kb[span, cols(head)]
            vals = vb[span, cols(head)]
            q = q_ref[rows, pair]
            r = lax.broadcasted_iota(jnp.int32, (128, width), 1) + 128 * half
            i = lax.broadcasted_iota(jnp.int32, (128, width), 0) + 128 * half
            allowed = (r >= low_ref[rows]) & (r <= i + WINDOW)
            outs = []
            for n in range(2):
                scores = lax.dot_general(
                    q[:, HEAD_SIZE * n : HEAD_SIZE * n + HEAD_SIZE],
                    keys,
                    (((1,), (1,)), ((), ())),
                    preferred_element_type=jnp.float32,
                )
                scores = jnp.where(allowed, scores, -1e30)
                peak = jnp.max(scores, axis=1, keepdims=True)
                expon = jnp.exp2((scores - peak) * FACTOR)
                total = jnp.sum(expon, axis=1, keepdims=True)
                mixed = jnp.dot(expon.astype(jnp.bfloat16), vals, preferred_element_type=jnp.float32)
                outs.append((mixed / total).astype(jnp.bfloat16))
            o_ref[rows, pair] = jnp.concatenate(outs, axis=1)

    def piece(i):
        return (z + ((i + 1) // 2) * (1 - 2 * (i % 2)) + 8) % 8

    def z_send(p, to_stage, step):
        ref = wv.at[core, p % 4, g, f, :, w_cols(p)]
        return remote(ref, ref, zs.at[to_stage], zr.at[to_stage], at_z(step))

    def f_copy(i, from_f, lane, step):
        p = piece(i)
        ref = wv.at[core, p % 4, g, (from_f + 4) % 4, :, w_cols(p)]
        return remote(ref, ref, fs.at[i, lane], fr.at[i, lane], at_f(step))

    def s_copy(i, from_g, lane, step):
        p = piece(i)
        ref = wv.at[core, p % 4, (from_g + 4) % 4, :, :, w_cols(p)]
        return remote(ref, ref, ss.at[i, lane], sr.at[i, lane], at_g(step))

    def s_half(i, from_g, lane, step):
        p = piece(i)
        ref = wv.at[core, p % 4, (from_g + 4) % 4, pl.ds(2 * (lane - 2), 2), :, w_cols(p)]
        return remote(ref, ref, ss.at[i, lane], sr.at[i, lane], at_g(step))

    def d_copy(i, from_core):
        p = piece(i)
        ref = wv.at[from_core, p % 4, :, :, :, w_cols(p)]
        return remote(ref, ref, ds.at[i], dr.at[i], partner)

    def out_copy(i, from_core):
        p = piece(i)
        where = (from_core, p % 4, slice(None), slice(None), slice(None), w_cols(p))
        return pltpu.make_async_copy(wv.at[where], wb.at[where], lw.at[from_core, i])

    def weight_tick(t):
        @pl.when(t == 0)
        def _():
            z_send(z, 1, 1).start()
            z_send(z, 2, -1).start()

        @pl.when((t > 0) & (t < STAGES))
        def _():
            z_send(piece(t), t, 1).wait_recv()

            @pl.when((t <= 4) | ((t == 5) & (core == 0)) | ((t == 6) & (core == 1)))
            def _():
                z_send(piece(t), jnp.minimum(t + 2, 7), 2 * (t % 2) - 1).start()

        @pl.when(t < STAGES)
        def _():
            f_copy(t, f, 0, 1).start()
            f_copy(t, f, 1, -1).start()

        @pl.when((t >= 1) & (t < STAGES + 1))
        def _():
            i = t - 1
            f_copy(i, f - 1, 0, 1).wait_recv()
            f_copy(i, f + 1, 1, -1).wait_recv()
            sign = 1 - 2 * (i % 2)
            f_copy(i, f - sign, 2, sign).start()

        @pl.when((t >= 2) & (t < STAGES + 2))
        def _():
            i = t - 2
            f_copy(i, f + 2, 2, 1).wait_recv()
            s_copy(i, g, 0, 1).start()
            s_copy(i, g, 1, -1).start()

        @pl.when((t >= 3) & (t < STAGES + 3))
        def _():
            i = t - 3
            s_copy(i, g - 1, 0, 1).wait_recv()
            s_copy(i, g + 1, 1, -1).wait_recv()
            s_half(i, g - 1, 2, 1).start()
            s_half(i, g + 1, 3, -1).start()

        @pl.when((t >= 4) & (t < STAGES + 4))
        def _():
            i = t - 4
            s_half(i, g + 2, 2, 1).wait_recv()
            s_half(i, g + 2, 3, -1).wait_recv()
            d_copy(i, core).start()
            out_copy(i, core).start()

        @pl.when((t >= 5) & (t < STAGES + 5))
        def _():
            i = t - 5
            d_copy(i, 1 - core).wait_recv()
            out_copy(i, 1 - core).start()

    kv_begin(0)

    def tick(t, _):
        weight_tick(t)

        @pl.when(t < CHUNKS - 1)
        def _():
            kv_begin(t + 1)

        @pl.when((t >= 1) & (t < CHUNKS + 1))
        def _():
            kv_near(t - 1)
            kv_far(t - 1)

        @pl.when((t >= 2) & (t < CHUNKS + 2))
        def _():
            kv_last(t - 2)

        @pl.when((t >= 3) & (t < CHUNKS + 3))
        def _():
            kv_done(t - 3)
            attend(t - 3)

        return 0

    lax.fori_loop(0, TICKS + 1, tick, 0)

    def finish(i, _):
        sent(0, i)

        @pl.when(to_opposite)
        def _():
            sent(1, i)

        sent(2, i)

        @pl.when(jnp.logical_not(b_second))
        def _():
            sent(3, i)

        @pl.when(b_first)
        def _():
            sent(4, i)

        @pl.when(jnp.logical_or(b_first, jnp.logical_and(a_second, jnp.logical_not(last_of_four))))
        def _():
            sent(5, i)

        d_copy(i, core).wait_send()
        for lane in range(3):
            f_copy(i, f, lane, 1).wait_send()
        for lane in range(2):
            s_copy(i, g, lane, 1).wait_send()
            s_half(i, g, lane + 2, 1).wait_send()
        out_copy(i, 0).wait()
        out_copy(i, 1).wait()

        @pl.when(i > 0)
        def _():
            z_send(piece(i), i, 1).wait_send()

        return 0

    lax.fori_loop(0, STAGES, finish, 0)


def exchange(lengths, queries, keys, values, weight):
    anyspace = pl.BlockSpec(memory_space=pl.ANY)
    vmem = pl.BlockSpec(memory_space=pltpu.VMEM)
    dma = pltpu.SemaphoreType.DMA
    return pl.pallas_call(
        exchange_kernel,
        out_shape=(
            jax.ShapeDtypeStruct((ROWS, QUERY_HEADS * HEAD_SIZE), jnp.bfloat16),
            jax.ShapeDtypeStruct((2, 4, 4, 4, 16, D), jnp.bfloat16),
        ),
        in_specs=[vmem, anyspace, anyspace, anyspace, anyspace],
        out_specs=(vmem, anyspace),
        scratch_shapes=[
            pltpu.VMEM((ROWS, QUERY_HEADS * HEAD_SIZE), jnp.bfloat16),
            pltpu.VMEM((WINDOW + ROWS, 1024), jnp.bfloat16),
            pltpu.VMEM((WINDOW + ROWS, 1024), jnp.bfloat16),
            pltpu.VMEM((2, 4, 4, 4, 16, D), jnp.bfloat16),
            pltpu.VMEM((ROWS, 1), jnp.int32),
            dma((4,)), dma((2, 8)),
            dma((8,)), dma((8,)),
            dma((8, 3)), dma((8, 3)),
            dma((8, 4)), dma((8, 4)),
            dma((8,)), dma((8,)),
            dma((6, CHUNKS, 2)), dma((4, CHUNKS, 2)),
        ],
        compiler_params=pltpu.CompilerParams(
            collective_id=0, has_side_effects=True, vmem_limit_bytes=56 * 1024 * 1024
        ),
        name="exchange",
    )(lengths, queries, keys, values, weight)


def low_bound(lengths, offset):
    row = lax.broadcasted_iota(jnp.int32, (64, 64), 0)
    col = lax.broadcasted_iota(jnp.int32, (64, 64), 1)
    starts_col = jnp.sum(jnp.where(col < row, lengths, 0), axis=1, keepdims=True)
    starts = jnp.sum(jnp.where(row == col, starts_col, 0), axis=0, keepdims=True)
    i = lax.broadcasted_iota(jnp.int32, (ROWS, 1), 0)
    begins = jnp.max(jnp.where(starts <= i + offset, starts, 0), axis=1, keepdims=True)
    return jnp.maximum(begins - offset + WINDOW, i + 1)


TILE = 768
TILES = D // TILE


def project_kernel(a_ref, w_ref, res_ref, gain_ref, o_ref, acc, square):
    n = pl.program_id(0)
    slabs = []
    for x in range(4):
        for y in range(4):
            for zl in range(4):
                slabs.append(w_ref[0, zl, y, x])
                slabs.append(w_ref[1, zl, x, y])
    weight = jnp.concatenate(slabs, axis=0)
    part = jnp.dot(a_ref[...], weight, preferred_element_type=jnp.float32)
    acc[n] = part
    here = jnp.sum(part * part, axis=1, keepdims=True)

    @pl.when(n == 0)
    def _():
        square[...] = here

    @pl.when(n > 0)
    def _():
        square[...] += here

    @pl.when(n == TILES - 1)
    def _():
        level = lax.rsqrt(square[...] * (1.0 / D) + 1e-06)
        for m in range(TILES):
            columns = slice(TILE * m, TILE * m + TILE)
            normed = gain_ref[:, columns] * acc[m] * level
            o_ref[:, columns] = (res_ref[:, columns].astype(jnp.float32) + normed).astype(jnp.bfloat16)


def project(attended, wb, residual, gain):
    return pl.pallas_call(
        project_kernel,
        grid=(TILES,),
        out_shape=jax.ShapeDtypeStruct((ROWS, D), jnp.bfloat16),
        in_specs=[
            pl.BlockSpec((ROWS, QUERY_HEADS * HEAD_SIZE), lambda n: (0, 0)),
            pl.BlockSpec((2, 4, 4, 4, 16, TILE), lambda n: (0, 0, 0, 0, 0, n)),
            pl.BlockSpec((ROWS, D), lambda n: (0, 0)),
            pl.BlockSpec((1, D), lambda n: (0, 0)),
        ],
        out_specs=pl.BlockSpec((ROWS, D), lambda n: (0, 0)),
        scratch_shapes=[
            pltpu.VMEM((TILES, ROWS, TILE), jnp.float32),
            pltpu.VMEM((ROWS, 1), jnp.float32),
        ],
        compiler_params=pltpu.CompilerParams(vmem_limit_bytes=48 * 1024 * 1024),
        name="project",
    )(attended, wb, residual, gain)


def shards(queries, key_rotated_rows, values, out_weight, residual, norm_gain, doc_lengths):
    attended, wb = exchange(doc_lengths.reshape(1, 64), queries, key_rotated_rows, values, out_weight)
    return project(attended, wb, residual, norm_gain.reshape(1, D))


def solution(mesh):
    rows = P(("seq", "fsdp"), None)
    in_specs = (rows, rows, rows, P("seq", "fsdp"), rows, P(), P())
    return jax.shard_map(shards, mesh=mesh, in_specs=in_specs, out_specs=rows, check_vma=False)
```

time: 164 us -> 143 us (0.87)
  Pallas kernels: 162 us -> 139 us
  local copies, waits for them, and re-layouts: 1.25 us -> 3.75 us
    pallas_call x3 -> x2, Pallas kernels: 162 us -> 139 us  [the longest x1 123 us: exchange(): pl.pallas_call(exchange_kernel, out_shape=(jax.ShapeDtypeStruct((ROWS, QU...]
    unnamed x6 -> x4, local copies, waits for them, and re-layouts: 1.23 us -> 3 us
where the time goes in v2:
time: 143 us; the launch traced here: 142 us
  Pallas kernels  139 us (97%)
  local copies, waits for them, and re-layouts  3.75 us (3%)
    pallas_call x1, Pallas kernels, exchange(): pl.pallas_call(exchange_kernel, out_shape=(jax.ShapeDtypeStruct((ROWS, QU...  123 us
    pallas_call x1, Pallas kernels, project(): pl.pallas_call(project_kernel, grid=(TILES,), out_shape=jax.ShapeDtypeStr...  15.3 us
    unnamed x4, local copies, waits for them, and re-layouts  3 us

profile of v2, /device:TPU:1, one launch (start us, length us, event | category | flops | bytes accessed | tf_op | source)
XLA Modules:
  0.0 142.5 jit_solution(16081963750995760721)
XLA Ops:
  0.0 0.8 reshape.7.gain_ref
  0.8 123.4 %exchange.1 = (bf16[256,2048]{1,0:T(8,128)(2,1)}, bf16[2,4,4,4,16,5376]{5,4,3,2,1,0:T(8,128)(2,1)}) custom-call(s32[1,64]{1,0:T(1,128)} %bitcast.1, bf16[256,2048]{1,0:T(8,128)(2,1)} %q_hbm.1, bf16[256,1024]{1,0:T(8,128)(2,1)} %k_ref.1, bf16[256,1024]{1,0:T(8,128)(2,1)} %v_ref.1, bf16[16,2688]{1,0:T(8,128)(2,1)} %w_ref.1), custom_call_target="tpu_custom_call" | custom-call | tf_op jit(solution)/shard_map/exchange/pallas_call | solution.py:378
  124.2 0.0 copy-start
  124.2 1.8 %copy-done = bf16[256,5376]{1,0:T(8,128)(2,1)S(1)} copy-done((bf16[256,5376]{1,0:T(8,128)(2,1)S(1)}, bf16[256,5376]{1,0:T(8,128)(2,1)}, u32[]{:S(2)}) %copy-start) | copy-done | bytes 2752536
  125.9 0.0 copy-start.1
  125.9 1.2 copy-done.1
  127.2 15.3 %project.1 = bf16[256,5376]{1,0:T(8,128)(2,1)} custom-call(bf16[256,2048]{1,0:T(8,128)(2,1)S(1)} %copy-done.1, bf16[2,4,4,4,16,5376]{5,4,3,2,1,0:T(8,128)(2,1)} %get-tuple-element.8.w_ref, bf16[256,5376]{1,0:T(8,128)(2,1)S(1)} %copy-done, f32[1,5376]{1,0:T(1,128)S(1)} %reshape.7.gain_ref), custom_call_target="tpu_custom_call" | custom-call | tf_op jit(solution)/shard_map/project/pallas_call | solution.py:451
Async XLA Ops:
  124.2 1.8 %copy-start = (bf16[256,5376]{1,0:T(8,128)(2,1)S(1)}, bf16[256,5376]{1,0:T(8,128)(2,1)}, u32[]{:S(2)}) copy-start(bf16[256,5376]{1,0:T(8,128)(2,1)} %res_ref.1) | copy-start | bytes 8257540
  125.9 1.2 copy-start.1
